TPU v7x, 32 devices: a whole 2x2x4 slice. The times are simulated.
32 devices in a mesh: pulse: 16 (over z, y, core), rng: 2 (over x).
Axes of the slice: x: 2, y: 2, z: 4, core: 2. Of those that a mesh axis runs over, the one named last changes fastest.
Arguments:
- raw_pulses: bfloat16 [2, 512, 8192], P(None, 'pulse', 'rng'), may hold values from -6 to 6
- azimuth_taps: float32 [2, 9], replicated, may hold values from -1.5 to 1.5
- range_taps: bfloat16 [2, 128], replicated, may hold values from -0.375 to 0.375
- steering: bfloat16 [2, 32, 32], replicated, may hold values from -0.75 to 0.75
- angle_mats: bfloat16 [4, 2, 32, 32], replicated, may hold values from -0.75 to 0.75
- range_resampler_matrices: bfloat16 [4, 2, 128, 128], replicated, may hold values from -0.375 to 0.375
- beam_phase: float32 [4, 64], replicated, may hold values from -3.140625 to 3.140625
- tap_blocks: int32 [4, 2, 64], P(None, None, 'rng'), may hold values from 0 to 62, as said below
Outputs:
- image: bfloat16 [2, 512, 8192], P(None, 'pulse', 'rng')
Inputs may be any that keep to these rules, and one draw needn't show every extreme that they name: tap_blocks[s, h, b] lies in the same aligned run of 32 range blocks as b and is never the last block of that run.
All inputs are finite; a program needn't handle non-finite values.
Results may differ from a plain program's by a relative error of at most 0.028.
Values may be sent and summed in bfloat16 or wider, within the bound.
A program may use at most 64 MiB of HBM per device.

v0:
```python
import jax
import jax.numpy as jnp
from jax import lax
from jax.sharding import PartitionSpec as P


def extended(cells, sides, width):
    for axis, dim in sides:
        count = lax.axis_size(axis)
        ends = count - 1
        head = lax.slice_in_dim(cells, 0, width, axis=dim)
        tail = lax.slice_in_dim(cells, cells.shape[dim] - width, cells.shape[dim], axis=dim)
        cells = jnp.concatenate(
            [
                lax.ppermute(tail, axis, [(i, (i + 1) % count) for i in range(ends)]),
                cells,
                lax.ppermute(head, axis, [((i + 1) % count, i) for i in range(ends)]),
            ],
            axis=dim,
        )
    return cells


def shifted(value, axis, steps):
    count = lax.axis_size(axis)
    leading, last = (max(0, -steps), min(count, count - steps))
    return lax.ppermute(value, axis, [(source, source + steps) for source in range(leading, last)])


def swapped(value, axis, apart):
    mask = 2**apart
    pairs = [(source, source ^ mask) for source in range(lax.axis_size(axis))]
    return lax.ppermute(value, axis, pairs)


def azimuth(padded, azimuth_taps, count):
    real_sum = jnp.zeros((count, padded.shape[2]), jnp.float32)
    imag_sum = jnp.zeros((count, padded.shape[2]), jnp.float32)
    for offset in range(azimuth_taps.shape[1]):
        window = lax.slice_in_dim(padded, offset, offset + count, axis=1).astype(jnp.float32)
        real_sum = (
            real_sum + azimuth_taps[0, offset] * window[0] - azimuth_taps[1, offset] * window[1]
        )
        imag_sum = (
            imag_sum + azimuth_taps[0, offset] * window[1] + azimuth_taps[1, offset] * window[0]
        )
    return jnp.stack([real_sum, imag_sum]).astype(jnp.bfloat16)


def complex_form(matrix):
    first = jnp.stack([matrix[0], matrix[1]], axis=1)
    second = jnp.stack([-matrix[1], matrix[0]], axis=1)
    return jnp.stack([first, second])


def toeplitz_pair(range_taps):
    width = range_taps.shape[1]
    rows = jnp.arange(width, dtype=jnp.int32)[:, None, None]
    cols = jnp.arange(width, dtype=jnp.int32)[None, :, None]
    lags = jnp.arange(width, dtype=jnp.int32)[None, None, :]
    spacing = cols - rows
    current_table = (spacing == lags).astype(jnp.float32)
    earlier_table = (spacing + width == lags).astype(jnp.float32)
    tap_values = range_taps.astype(jnp.float32)
    current = jnp.einsum("ck,ijk->cij", tap_values, current_table).astype(jnp.bfloat16)
    earlier = jnp.einsum("ck,ijk->cij", tap_values, earlier_table).astype(jnp.bfloat16)
    return jnp.stack([complex_form(current), complex_form(earlier)])


def resample(subimage, angle_set, range_pair, phase_ramp_row, tap_rows, sector, sign, block_start):
    beams = subimage.shape[1]
    width = range_pair.shape[1]
    matrix = lax.dynamic_index_in_dim(angle_set, sector, 0, keepdims=False)
    turned = jnp.einsum("ab,cbr->car", matrix, subimage, preferred_element_type=jnp.float32).astype(
        jnp.bfloat16
    )
    blocked = turned.reshape(2, beams, -1, width)
    local_blocks = blocked.shape[2]
    chosen = lax.dynamic_index_in_dim(tap_rows, sector, 0, keepdims=False) - block_start
    picks = jnp.stack([chosen, chosen + 1])
    positions = jnp.arange(local_blocks, dtype=jnp.int32)
    selector = (picks[:, :, None] == positions[None, None, :]).astype(jnp.bfloat16)
    picked = jnp.einsum(
        "kob,cabi->kcaoi", selector, blocked, preferred_element_type=jnp.float32
    ).astype(jnp.bfloat16)
    moved = jnp.einsum("kcani,kij->canj", picked, range_pair, preferred_element_type=jnp.float32)
    moved = moved.reshape(2, beams, -1)
    angle = sign * lax.dynamic_slice_in_dim(phase_ramp_row, sector * beams, beams)[:, None]
    cosine = jnp.cos(angle)
    sine = jnp.sin(angle)
    return jnp.stack([moved[0] * cosine - moved[1] * sine, moved[0] * sine + moved[1] * cosine])


def local(
    raw_pulses,
    azimuth_taps,
    range_taps,
    steering,
    angle_mats,
    range_resampler_matrices,
    beam_phase,
    tap_blocks,
):
    count = raw_pulses.shape[1]
    local_bins = raw_pulses.shape[2]
    width = range_taps.shape[1]
    local_blocks = local_bins // width
    rim_width = azimuth_taps.shape[1] // 2
    padded = extended(raw_pulses, (("pulse", 1),), rim_width)
    filtered = azimuth(padded, azimuth_taps, count)
    lower_rim = shifted(filtered[:, :, local_bins - width :], "rng", 1)
    blocked = filtered.reshape(2, count, local_blocks, width)
    earlier = jnp.concatenate([lower_rim[:, :, None, :], blocked[:, :, :-1]], axis=2)
    weights = toeplitz_pair(range_taps)
    pulse_compressed_data = jnp.einsum(
        "bcpni,bcioj->opnj",
        jnp.stack([blocked, earlier]),
        weights,
        preferred_element_type=jnp.float32,
    )
    pulse_compressed_data = pulse_compressed_data.astype(jnp.bfloat16).reshape(2, count, local_bins)
    real_component = jnp.dot(
        steering[0], pulse_compressed_data[0], preferred_element_type=jnp.float32
    ) - jnp.dot(steering[1], pulse_compressed_data[1], preferred_element_type=jnp.float32)
    imaginary_component = jnp.dot(
        steering[0], pulse_compressed_data[1], preferred_element_type=jnp.float32
    ) + jnp.dot(steering[1], pulse_compressed_data[0], preferred_element_type=jnp.float32)
    subimage = jnp.stack([real_component, imaginary_component]).astype(jnp.bfloat16)
    block_start = lax.axis_index("rng") * local_blocks
    member = lax.axis_index("pulse")
    for section in range(lax.axis_size("pulse").bit_length() - 1):
        parity = member // 2**section % 2
        sign = (2 * parity - 1).astype(jnp.float32)
        outgoing = resample(
            subimage,
            angle_mats[section],
            range_resampler_matrices[section],
            beam_phase[section],
            tap_blocks[section],
            1 - parity,
            sign,
            block_start,
        ).astype(jnp.bfloat16)
        self_contribution = resample(
            subimage,
            angle_mats[section],
            range_resampler_matrices[section],
            beam_phase[section],
            tap_blocks[section],
            parity,
            sign,
            block_start,
        )
        incoming = swapped(outgoing, "pulse", section)
        subimage = (self_contribution + incoming.astype(jnp.float32)).astype(jnp.bfloat16)
    return subimage


def solution(mesh):
    return jax.shard_map(
        local,
        mesh=mesh,
        in_specs=(P(None, "pulse", "rng"), P(), P(), P(), P(), P(), P(), P(None, None, "rng")),
        out_specs=P(None, "pulse", "rng"),
        check_vma=False,
    )
```

profile of v0, /device:TPU:6, one launch (start us, length us, event | category | flops | bytes accessed | tf_op | source)
XLA Modules:
  0.0 122.4 jit_solution(7445991321715893954)
XLA Ops:
  0.0 1.0 fusion.225
  1.0 1.9 %collective-permute-start = (bf16[2,4,4096]{2,1,0:T(4,128)(2,1)S(1)}, bf16[2,4,4096]{2,1,0:T(4,128)(2,1)S(1)}, u32[]{:S(2)}, u32[]{:S(2)}) collective-permute-start(bf16[2,4,4096]{2,1,0:T(4,128)(2,1)S(1)} %get-tuple-element.69), channel_id=1, source_target_pairs={{0,2},{2,4},{4,6},{6,8},{8,10},{10,12},{12,14},{14,16},{16,18},{18... | collective-permute-start | bytes 196616 | tf_op jit(solution)/shard_map/ppermute | solution.py:15
  3.0 3.6 %collective-permute-start.1 = (bf16[2,4,4096]{2,1,0:T(4,128)(2,1)S(1)}, bf16[2,4,4096]{2,1,0:T(4,128)(2,1)S(1)}, u32[]{:S(2)}, u32[]{:S(2)}) collective-permute-start(bf16[2,4,4096]{2,1,0:T(4,128)(2,1)S(1)} %get-tuple-element.70), channel_id=1, source_target_pairs={{2,0},{4,2},{6,4},{8,6},{10,8},{12,10},{14,12},{16,14},{18,16},{20... | collective-permute-start | bytes 196616 | tf_op jit(solution)/shard_map/ppermute | solution.py:17
  6.8 2.0 %fusion.231 = (f32[1,1]{1,0:T(1,128)}, f32[1,1]{1,0:T(1,128)}, f32[1,1]{1,0:T(1,128)}, f32[1,1]{1,0:T(1,128)}, f32[1,1]{1,0:T(1,128)}, /*index=5*/f32[1,1]{1,0:T...) fusion(f32[2,9]{1,0:T(2,128)} %param.9), kind=kLoop, calls=%fused_computation.320 | loop fusion | bytes 144 | tf_op jit(solution)/shard_map/slice | solution.py:42
  8.9 3.7 %fusion.34 = bf16[2,128,128]{2,0,1:T(2,128)(2,1)S(1)} fusion(s32[128,128]{1,0:T(8,128)S(1)} %iota_subtract_fusion, bf16[2,128]{1,0:T(2,128)(2,1)S(1)} %copy-done), kind=kOutput, calls=%fused_computation.54 | convolution fusion | flops 10518528 | bytes 131584 | tf_op jit(solution)/shard_map/ck,ijk->cij/dot_general | solution.py:65
  12.7 3.7 %fusion.35 = bf16[2,128,128]{2,0,1:T(2,128)(2,1)S(1)} fusion(s32[128,128]{1,0:T(8,128)S(1)} %broadcast_add_fusion, bf16[2,128]{1,0:T(2,128)(2,1)S(1)} %copy-done), kind=kOutput, calls=%fused_computation.55 | convolution fusion | flops 10518528 | bytes 131584 | tf_op jit(solution)/shard_map/ck,ijk->cij/dot_general | solution.py:66
  18.7 12.1 %subtract_convert_fusion.4 = bf16[1,32,4096]{2,1,0:T(8,128)(2,1)S(1)} fusion(f32[2,32,4096]{2,1,0:T(8,128)S(1)} %get-tuple-element.58, f32[2,32,4096]{2,1,0:T(8,128)S(1)} %get-tuple-element.59, f32[2,32,4096]{2,1,0:T(8,128)S(1)} %get-tuple-element.60, f32[2,32,4096]{2,1,0:T(8,128)S(1)} %get-tuple-element.57, f32[2,32,4096]{2,1,0:T(8,128)S(1)} %get-tuple-element.67, ...), kind=kLoop, calls=%fused_computation.123 | loop fusion | flops 4718592 | bytes 9699400 | tf_op jit(solution)/shard_map/convert.23
  30.8 12.1 %add_convert_fusion.4 = bf16[1,32,4096]{2,1,0:T(8,128)(2,1)S(1)} fusion(f32[2,32,4096]{2,1,0:T(8,128)S(1)} %get-tuple-element.58, f32[2,32,4096]{2,1,0:T(8,128)S(1)} %get-tuple-element.59, f32[2,32,4096]{2,1,0:T(8,128)S(1)} %get-tuple-element.60, f32[2,32,4096]{2,1,0:T(8,128)S(1)} %get-tuple-element.57, f32[2,32,4096]{2,1,0:T(8,128)S(1)} %get-tuple-element.67, ...), kind=kLoop, calls=%fused_computation.122 | loop fusion | flops 4718592 | bytes 9699400 | tf_op jit(solution)/shard_map/convert.22
  42.9 1.5 %collective-permute-start.2 = (bf16[2,32,128]{2,1,0:T(8,128)(2,1)S(1)}, bf16[2,32,128]{2,1,0:T(8,128)(2,1)S(1)}, u32[]{:S(2)}, u32[]{:S(2)}) collective-permute-start(bf16[2,32,128]{2,1,0:T(8,128)(2,1)S(1)} %pad_maximum_fusion.9), channel_id=1, source_target_pairs={{0,1},{2,3},{4,5},{6,7},{8,9},{10,11},{12,13},{14,15},{16,17},{18,... | collective-permute-start | bytes 49160 | tf_op jit(solution)/shard_map/ppermute | solution.py:27
  44.6 4.0 %collective-permute-done.2 = bf16[2,32,128]{2,1,0:T(8,128)(2,1)S(1)} collective-permute-done((bf16[2,32,128]{2,1,0:T(8,128)(2,1)S(1)}, bf16[2,32,128]{2,1,0:T(8,128)(2,1)S(1)}, u32[]{:S(2)}, u32[]{:S(2)}) %collective-permute-start.2) | collective-permute-done | bytes 16416 | tf_op jit(solution)/shard_map/ppermute | solution.py:27
  52.1 0.8 fusion.13
  53.4 0.8 pad_maximum_fusion.3
  54.4 0.8 fusion.10
  57.5 0.9 fusion.220
  58.4 1.1 squeeze.298
  59.9 0.8 pad_maximum_fusion.4
  61.1 0.8 fusion.16
  62.4 12.5 %collective-permute-done.4 = bf16[2,32,4096]{2,1,0:T(8,128)(2,1)S(1)} collective-permute-done((bf16[2,32,4096]{2,1,0:T(8,128)(2,1)}, bf16[2,32,4096]{2,1,0:T(8,128)(2,1)S(1)}, u32[]{:S(2)}, u32[]{:S(2)}) %collective-permute-start.4) | collective-permute-done | bytes 524320 | tf_op jit(solution)/shard_map/ppermute | solution.py:33
  75.3 0.8 fusion.25
  76.1 0.9 fusion.218
  76.9 1.1 squeeze.305
  78.4 0.8 pad_maximum_fusion.5
  79.2 1.6 %collective-permute-start.5 = (bf16[2,32,4096]{2,1,0:T(8,128)(2,1)}, bf16[2,32,4096]{2,1,0:T(8,128)(2,1)S(1)}, u32[]{:S(2)}, u32[]{:S(2)}) collective-permute-start(bf16[2,32,4096]{2,1,0:T(8,128)(2,1)} %pad_maximum_fusion.5), channel_id=1, source_target_pairs={{0,8},{2,10},{4,12},{6,14},{8,0},{10,2},{12,4},{14,6},{16,24},{18,... | collective-permute-start | bytes 1572872 | tf_op jit(solution)/shard_map/ppermute | solution.py:33
  82.4 10.1 %collective-permute-done.5 = bf16[2,32,4096]{2,1,0:T(8,128)(2,1)S(1)} collective-permute-done((bf16[2,32,4096]{2,1,0:T(8,128)(2,1)}, bf16[2,32,4096]{2,1,0:T(8,128)(2,1)S(1)}, u32[]{:S(2)}, u32[]{:S(2)}) %collective-permute-start.5) | collective-permute-done | bytes 524320 | tf_op jit(solution)/shard_map/ppermute | solution.py:33
  92.9 0.8 fusion.31
  93.7 0.9 fusion.216
  94.6 1.1 squeeze.312
  96.0 0.8 pad_maximum_fusion.6
  96.9 2.6 %collective-permute-start.6 = (bf16[2,32,4096]{2,1,0:T(8,128)(2,1)}, bf16[2,32,4096]{2,1,0:T(8,128)(2,1)S(1)}, u32[]{:S(2)}, u32[]{:S(2)}) collective-permute-start(bf16[2,32,4096]{2,1,0:T(8,128)(2,1)} %pad_maximum_fusion.6), channel_id=1, source_target_pairs={{0,16},{2,18},{4,20},{6,22},{8,24},{10,26},{12,28},{14,30},{16,0},... | collective-permute-start | bytes 1572872 | tf_op jit(solution)/shard_map/ppermute | solution.py:33
  99.8 0.8 fusion.28
  101.1 20.4 %collective-permute-done.6 = bf16[2,32,4096]{2,1,0:T(8,128)(2,1)S(1)} collective-permute-done((bf16[2,32,4096]{2,1,0:T(8,128)(2,1)}, bf16[2,32,4096]{2,1,0:T(8,128)(2,1)S(1)}, u32[]{:S(2)}, u32[]{:S(2)}) %collective-permute-start.6) | collective-permute-done | bytes 524320 | tf_op jit(solution)/shard_map/ppermute | solution.py:33
  121.5 0.9 fusion.44
  (103 shorter events, 13.5 us)
Async XLA Ops:
  0.0 8.9 %copy-start = (bf16[2,128]{1,0:T(2,128)(2,1)S(1)}, bf16[2,128]{1,0:T(2,128)(2,1)}, u32[]{:S(2)}) copy-start(bf16[2,128]{1,0:T(2,128)(2,1)} %param.10) | copy-start | bytes 1540
  1.0 16.2 %collective-permute-start = (bf16[2,4,4096]{2,1,0:T(4,128)(2,1)S(1)}, bf16[2,4,4096]{2,1,0:T(4,128)(2,1)S(1)}, u32[]{:S(2)}, u32[]{:S(2)}) collective-permute-start(bf16[2,4,4096]{2,1,0:T(4,128)(2,1)S(1)} %get-tuple-element.69), channel_id=1, source_target_pairs={{0,2},{2,4},{4,6},{6,8},{8,10},{10,12},{12,14},{14,16},{16,18},{18... | collective-permute-start | bytes 196616 | tf_op jit(solution)/shard_map/ppermute | solution.py:15
  3.0 15.2 %collective-permute-start.1 = (bf16[2,4,4096]{2,1,0:T(4,128)(2,1)S(1)}, bf16[2,4,4096]{2,1,0:T(4,128)(2,1)S(1)}, u32[]{:S(2)}, u32[]{:S(2)}) collective-permute-start(bf16[2,4,4096]{2,1,0:T(4,128)(2,1)S(1)} %get-tuple-element.70), channel_id=1, source_target_pairs={{2,0},{4,2},{6,4},{8,6},{10,8},{12,10},{14,12},{16,14},{18,16},{20... | collective-permute-start | bytes 196616 | tf_op jit(solution)/shard_map/ppermute | solution.py:17
  12.7 3.9 %copy-start.4 = (bf16[4,2,32,32]{3,2,1,0:T(8,128)(2,1)S(1)}, bf16[4,2,32,32]{3,2,1,0:T(8,128)(2,1)}, u32[]{:S(2)}) copy-start(bf16[4,2,32,32]{3,2,1,0:T(8,128)(2,1)} %param.12) | copy-start | bytes 49156
  12.7 3.9 %copy-start.5 = (s32[4,2,32]{2,1,0:T(2,128)S(1)}, s32[4,2,32]{2,1,0:T(2,128)}, u32[]{:S(2)}) copy-start(s32[4,2,32]{2,1,0:T(2,128)} %param.15) | copy-start | bytes 3076
  12.7 3.9 %copy-start.6 = (f32[4,64]{1,0:T(4,128)S(1)}, f32[4,64]{1,0:T(4,128)}, u32[]{:S(2)}) copy-start(f32[4,64]{1,0:T(4,128)} %param.14) | copy-start | bytes 3076
  16.4 1.0 copy-start.2
  42.9 5.6 %collective-permute-start.2 = (bf16[2,32,128]{2,1,0:T(8,128)(2,1)S(1)}, bf16[2,32,128]{2,1,0:T(8,128)(2,1)S(1)}, u32[]{:S(2)}, u32[]{:S(2)}) collective-permute-start(bf16[2,32,128]{2,1,0:T(8,128)(2,1)S(1)} %pad_maximum_fusion.9), channel_id=1, source_target_pairs={{0,1},{2,3},{4,5},{6,7},{8,9},{10,11},{12,13},{14,15},{16,17},{18,... | collective-permute-start | bytes 49160 | tf_op jit(solution)/shard_map/ppermute | solution.py:27
  49.3 0.7 copy-start.3
  51.2 1.0 copy-start.1
  54.3 2.1 %collective-permute-start.3 = (bf16[2,32,4096]{2,1,0:T(8,128)(2,1)}, bf16[2,32,4096]{2,1,0:T(8,128)(2,1)S(1)}, u32[]{:S(2)}, u32[]{:S(2)}) collective-permute-start(bf16[2,32,4096]{2,1,0:T(8,128)(2,1)} %pad_maximum_fusion.3), channel_id=1, source_target_pairs={{0,2},{2,0},{4,6},{6,4},{8,10},{10,8},{12,14},{14,12},{16,18},{18,... | collective-permute-start | bytes 1572872 | tf_op jit(solution)/shard_map/ppermute | solution.py:33
  60.7 14.2 %collective-permute-start.4 = (bf16[2,32,4096]{2,1,0:T(8,128)(2,1)}, bf16[2,32,4096]{2,1,0:T(8,128)(2,1)S(1)}, u32[]{:S(2)}, u32[]{:S(2)}) collective-permute-start(bf16[2,32,4096]{2,1,0:T(8,128)(2,1)} %pad_maximum_fusion.4), channel_id=1, source_target_pairs={{0,4},{2,6},{4,0},{6,2},{8,12},{10,14},{12,8},{14,10},{16,20},{18,... | collective-permute-start | bytes 1572872 | tf_op jit(solution)/shard_map/ppermute | solution.py:33
  79.2 13.3 %collective-permute-start.5 = (bf16[2,32,4096]{2,1,0:T(8,128)(2,1)}, bf16[2,32,4096]{2,1,0:T(8,128)(2,1)S(1)}, u32[]{:S(2)}, u32[]{:S(2)}) collective-permute-start(bf16[2,32,4096]{2,1,0:T(8,128)(2,1)} %pad_maximum_fusion.5), channel_id=1, source_target_pairs={{0,8},{2,10},{4,12},{6,14},{8,0},{10,2},{12,4},{14,6},{16,24},{18,... | collective-permute-start | bytes 1572872 | tf_op jit(solution)/shard_map/ppermute | solution.py:33
  96.9 24.6 %collective-permute-start.6 = (bf16[2,32,4096]{2,1,0:T(8,128)(2,1)}, bf16[2,32,4096]{2,1,0:T(8,128)(2,1)S(1)}, u32[]{:S(2)}, u32[]{:S(2)}) collective-permute-start(bf16[2,32,4096]{2,1,0:T(8,128)(2,1)} %pad_maximum_fusion.6), channel_id=1, source_target_pairs={{0,16},{2,18},{4,20},{6,22},{8,24},{10,26},{12,28},{14,30},{16,0},... | collective-permute-start | bytes 1572872 | tf_op jit(solution)/shard_map/ppermute | solution.py:33
where the time goes:
time: 125 us; the launch traced here: 122 us
  waiting for transfers between devices  47.8 us (38%)
  other arithmetic  31.9 us (26%)
  matrix products  17.1 us (14%)
  local copies, waits for them, and re-layouts  13.3 us (11%)
  starting transfers between devices  11.2 us (9%)
    ppermute x4, waiting for transfers between devices, swapped(): return lax.ppermute(value, axis, pairs)  43.8 us
    another operation x6, other arithmetic  24.9 us
    dot_general x8, matrix products, resample(): jnp.einsum('kcani,kij->canj', picked, range_pair, preferred_element_type=...  6.23 us
    ppermute x4, starting transfers between devices, swapped(): return lax.ppermute(value, axis, pairs)  4.16 us
    ppermute x1, waiting for transfers between devices, shifted(): lax.ppermute(value, axis, [(source, source + steps) for source in range(l...  4.01 us
    squeeze x8, local copies, waits for them, and re-layouts, resample(): moved[0] * cosine - moved[1] * sine  3.91 us
    dot_general x1, matrix products, toeplitz_pair(): jnp.einsum('ck,ijk->cij', tap_values, current_table).astype(jnp.bfloat16)  3.69 us
    dot_general x1, matrix products, toeplitz_pair(): jnp.einsum('ck,ijk->cij', tap_values, earlier_table).astype(jnp.bfloat16)  3.69 us
  transfers between devices with their start and end apart: 7, of which 5 were waited for; matrix products, arithmetic and copies ran while one was open for 14% of the time, Pallas kernels for 0%

commit v1 on v0

v1 whole, which is shorter than its diff:
```python
import functools

import jax
import jax.numpy as jnp
from jax import lax
from jax.experimental import pallas as pl
from jax.experimental.pallas import tpu as pltpu
from jax.sharding import PartitionSpec as P

MESH = pl.DeviceIdType.MESH
F32 = jnp.float32
BF16 = jnp.bfloat16


def iota(shape, dim):
    return lax.broadcasted_iota(jnp.int32, shape, dim)


def mm(a, b):
    return jnp.dot(a, b, preferred_element_type=F32)


def placement(rows, cols, offset):
    return (iota((rows, cols), 1) == iota((rows, cols), 0) + offset).astype(BF16)


def azimuth_matrix(az, count, half):
    taps = 2 * half + 1
    shape = (2 * count, 2 * count + 4 * half)
    row, col = iota(shape, 0), iota(shape, 1)
    upper = row >= count
    pulse = jnp.where(upper, row - count, row)
    own = 2 * count
    low, high = own + 2 * half, own + 4 * half
    part = jnp.where(
        col < own,
        (col >= count).astype(jnp.int32),
        jnp.where(col < low, (col >= own + half).astype(jnp.int32), (col >= low + half).astype(jnp.int32)),
    )
    source = jnp.where(
        col < own,
        col - count * part,
        jnp.where(col < low, col - own - half * part - half, col - low - half * part + count),
    )
    lag = source - pulse + half
    same = upper == (part == 1)
    total = jnp.zeros(shape, F32)
    for k in range(taps):
        re, im = az[0, k], az[1, k]
        value = jnp.where(same, re, jnp.where(upper, im, -im))
        total = total + jnp.where(lag == k, value, 0.0)
    return total


def toeplitz(taps_row, width):
    rows = jnp.broadcast_to(taps_row, (width, width))
    return pltpu.roll(rows, 0, 1, stride=1, stride_axis=0)


def kernel(n, nr, raw, az, rt, st, am, rr, bp, tb, out,
           edge_out, edge_in, rim_out, rim_in, filt, x, turned, sendb, recvb, own, cs, w,
           edge_send, edge_recv, rim_send, rim_recv, send_sem, recv_sem):
    me, rn = lax.axis_index("pulse"), lax.axis_index("rng")
    count, bins = raw.shape[1], raw.shape[2]
    width = rt.shape[1]
    blocks = bins // width
    half = az.shape[1] // 2
    sections = n.bit_length() - 1
    chunks = sendb.shape[1]
    span = bins // chunks
    per = span // width

    def partner(s):
        mask = 2**s
        return me + mask - 2 * mask * ((me // mask) % 2)

    barrier = pltpu.get_barrier_semaphore()
    for s in range(sections):
        pl.semaphore_signal(barrier, inc=1, device_id=(partner(s), rn), device_id_type=MESH)
    for cond, target in ((me > 0, (me - 1, rn)), (me < n - 1, (me + 1, rn)),
                         (rn > 0, (me, rn - 1)), (rn < nr - 1, (me, rn + 1))):
        @pl.when(cond)
        def _(target=target):
            pl.semaphore_signal(barrier, inc=1, device_id=target, device_id_type=MESH)
    arrivals = (sections + (me > 0).astype(jnp.int32) + (me < n - 1).astype(jnp.int32)
                + (rn > 0).astype(jnp.int32) + (rn < nr - 1).astype(jnp.int32))

    shape = (4 * half, 2 * count)
    row, col = iota(shape, 0), iota(shape, 1)
    tail = row >= 2 * half
    local = jnp.where(tail, row - 2 * half, row)
    second = (local >= half).astype(jnp.int32)
    pick = local - half * second + jnp.where(tail, count - half, 0) + count * second
    chooser = (col == pick).astype(BF16)
    for c in range(chunks):
        cols = slice(c * span, (c + 1) * span)
        both = jnp.concatenate([raw[0, :, cols], raw[1, :, cols]], axis=0)
        edges = mm(chooser, both)
        edge_out[0, :, cols] = edges[: 2 * half].astype(BF16)
        edge_out[1, :, cols] = edges[2 * half :].astype(BF16)

    pl.semaphore_wait(barrier, arrivals)

    to_low = pltpu.make_async_remote_copy(
        edge_out.at[0], edge_in.at[1], edge_send.at[0], edge_recv.at[1],
        device_id=(me - 1, rn), device_id_type=MESH)
    to_high = pltpu.make_async_remote_copy(
        edge_out.at[1], edge_in.at[0], edge_send.at[1], edge_recv.at[0],
        device_id=(me + 1, rn), device_id_type=MESH)

    @pl.when(me > 0)
    def _():
        to_low.start()

    @pl.when(me < n - 1)
    def _():
        to_high.start()

    p0, p1 = placement(count, 2 * count, 0), placement(count, 2 * count, count)
    s_re, s_im = st[0], st[1]
    steer = jnp.concatenate([mm(s_re, p0) - mm(s_im, p1), mm(s_im, p0) + mm(s_re, p1)], axis=0)
    mix = jnp.dot(steer, azimuth_matrix(az, count, half), precision=lax.Precision.HIGHEST,
                  preferred_element_type=F32)
    first = mix.astype(BF16)
    rest = mix - first.astype(F32)
    second_part = rest.astype(BF16)
    third_part = (rest - second_part.astype(F32)).astype(BF16)
    taps = rt[...].astype(F32)
    rows, cols_ = iota((width, width), 0), iota((width, width), 1)
    full = [toeplitz(taps[c : c + 1], width) for c in range(2)]
    for e, keep in enumerate((cols_ >= rows, cols_ < rows)):
        m0, m1 = (jnp.where(keep, f, 0.0) for f in full)
        w[(2 * e) * width : (2 * e + 1) * width, :width] = m0.astype(BF16)
        w[(2 * e) * width : (2 * e + 1) * width, width:] = m1.astype(BF16)
        w[(2 * e + 1) * width : (2 * e + 2) * width, :width] = (-m1).astype(BF16)
        w[(2 * e + 1) * width : (2 * e + 2) * width, width:] = m0.astype(BF16)
    beams = am.shape[2]
    for s in range(sections):
        parity = (me // 2**s) % 2
        sign = (2 * parity - 1).astype(F32)
        for i, sector in enumerate((1 - parity, parity)):
            phases = jnp.broadcast_to(bp[s : s + 1, :], (beams, 2 * beams))
            hit = iota((beams, 2 * beams), 1) == iota((beams, 2 * beams), 0) + sector * beams
            angle = sign * jnp.sum(jnp.where(hit, phases, 0.0), axis=1, keepdims=True)
            angle = jnp.broadcast_to(angle, (beams, width))
            cs[s, i, 0] = jnp.cos(angle)
            cs[s, i, 1] = jnp.sin(angle)

    @pl.when(me == 0)
    def _():
        edge_in[0] = jnp.zeros(edge_in.shape[1:], BF16)

    @pl.when(me == n - 1)
    def _():
        edge_in[1] = jnp.zeros(edge_in.shape[1:], BF16)

    @pl.when(me > 0)
    def _():
        to_high.wait_recv()

    @pl.when(me < n - 1)
    def _():
        to_low.wait_recv()

    to_right = pltpu.make_async_remote_copy(
        rim_out, rim_in, rim_send, rim_recv, device_id=(me, rn + 1), device_id_type=MESH)
    for c in reversed(range(chunks)):
        cols = slice(c * span, (c + 1) * span)
        gathered = jnp.concatenate([raw[0, :, cols], raw[1, :, cols], edge_in[0, :, cols], edge_in[1, :, cols]], axis=0)
        value = (mm(first, gathered) + mm(second_part, gathered) + mm(third_part, gathered)).astype(BF16)
        for j in range(per):
            b = c * per + j + 1
            for part in range(2):
                filt[part, b * count : (b + 1) * count, :] = value[
                    part * count : (part + 1) * count, j * width : (j + 1) * width]
        if c == chunks - 1:
            for part in range(2):
                rim_out[part] = value[part * count : (part + 1) * count, span - width :]

            @pl.when(rn < nr - 1)
            def _():
                to_right.start()

    @pl.when(rn == 0)
    def _():
        filt[:, :count, :] = jnp.zeros((2, count, width), BF16)

    @pl.when(rn > 0)
    def _():
        to_right.wait_recv()
        filt[:, :count, :] = rim_in[...]

    weights = w[...]
    for c in range(chunks):
        r0 = c * per * count
        r1 = r0 + per * count
        lhs = jnp.concatenate(
            [filt[0, r0 + count : r1 + count, :], filt[1, r0 + count : r1 + count, :],
             filt[0, r0:r1, :], filt[1, r0:r1, :]], axis=1)
        res = mm(lhs, weights).astype(BF16)
        for j in range(per):
            b = c * per + j
            for part in range(2):
                x[part * count : (part + 1) * count, b * width : (b + 1) * width] = res[
                    j * count : (j + 1) * count, part * width : (part + 1) * width]

    start = rn * blocks
    for s in range(sections):
        parity = (me // 2**s) % 2
        sectors = (1 - parity, parity)
        a_out, a_own = am[s, 1 - parity], am[s, parity]
        a2 = jnp.concatenate([mm(a_out, p0), mm(a_out, p1), mm(a_own, p0), mm(a_own, p1)], axis=0).astype(BF16)
        for c in range(chunks):
            value = mm(a2, x[:, c * span : (c + 1) * span]).astype(BF16)
            for j in range(per):
                for i in range(2):
                    turned[i, c * per + j] = value[
                        i * 2 * beams : (i + 1) * 2 * beams, j * width : (j + 1) * width]
        pair = jnp.concatenate([rr[s, 0], rr[s, 1]], axis=0)

        def moved(i, c):
            lhs = []
            for j in range(per):
                t = jnp.maximum(tb[s, sectors[i], c * per + j] - start, 0)
                lhs.append(jnp.concatenate([turned[i, t], turned[i, t + 1]], axis=1))
            res = mm(jnp.concatenate(lhs, axis=0), pair)
            cosine, sine = cs[s, i, 0], cs[s, i, 1]
            for j in range(per):
                re = res[2 * j * beams : (2 * j + 1) * beams]
                im = res[(2 * j + 1) * beams : (2 * j + 2) * beams]
                yield j, re * cosine - im * sine, re * sine + im * cosine

        copies = []
        for c in range(chunks):
            for j, re, im in moved(0, c):
                sendb[s, c, :beams, j * width : (j + 1) * width] = re.astype(BF16)
                sendb[s, c, beams:, j * width : (j + 1) * width] = im.astype(BF16)
            copy = pltpu.make_async_remote_copy(
                sendb.at[s, c], recvb.at[s, c], send_sem.at[s, c], recv_sem.at[s, c],
                device_id=(partner(s), rn), device_id_type=MESH)
            copy.start()
            copies.append(copy)
        for c in range(chunks):
            for j, re, im in moved(1, c):
                b = c * per + j
                own[:beams, b * width : (b + 1) * width] = re
                own[beams:, b * width : (b + 1) * width] = im
        for c in range(chunks):
            copies[c].wait_recv()
            cols = slice(c * span, (c + 1) * span)
            merged = (own[:, cols] + recvb[s, c].astype(F32)).astype(BF16)
            if s == sections - 1:
                out[0, :, cols] = merged[:beams]
                out[1, :, cols] = merged[beams:]
            else:
                x[:, cols] = merged
        for copy in copies:
            copy.wait_send()

    @pl.when(me > 0)
    def _():
        to_low.wait_send()

    @pl.when(me < n - 1)
    def _():
        to_high.wait_send()

    @pl.when(rn < nr - 1)
    def _():
        to_right.wait_send()


def solution(mesh):
    n, nr = mesh.shape["pulse"], mesh.shape["rng"]

    def local(raw_pulses, azimuth_taps, range_taps, steering, angle_mats,
              range_resampler_matrices, beam_phase, tap_blocks):
        count, bins = raw_pulses.shape[1:]
        width = range_taps.shape[1]
        half = azimuth_taps.shape[1] // 2
        blocks = bins // width
        sections = n.bit_length() - 1
        chunks = 4
        rows = 2 * count
        vmem = pl.BlockSpec(memory_space=pltpu.VMEM)
        smem = pl.BlockSpec(memory_space=pltpu.SMEM)
        dma = pltpu.SemaphoreType.DMA
        return pl.pallas_call(
            functools.partial(kernel, n, nr),
            out_shape=jax.ShapeDtypeStruct((2, count, bins), BF16),
            in_specs=[vmem, smem, vmem, vmem, vmem, vmem, vmem, smem],
            out_specs=vmem,
            scratch_shapes=[
                pltpu.VMEM((2, 2 * half, bins), BF16),
                pltpu.VMEM((2, 2 * half, bins), BF16),
                pltpu.VMEM((2, count, width), BF16),
                pltpu.VMEM((2, count, width), BF16),
                pltpu.VMEM((2, (blocks + 1) * count, width), BF16),
                pltpu.VMEM((rows, bins), BF16),
                pltpu.VMEM((2, blocks, rows, width), BF16),
                pltpu.VMEM((sections, chunks, rows, bins // chunks), BF16),
                pltpu.VMEM((sections, chunks, rows, bins // chunks), BF16),
                pltpu.VMEM((rows, bins), F32),
                pltpu.VMEM((sections, 2, 2, count, width), F32),
                pltpu.VMEM((4 * width, 2 * width), BF16),
                dma((2,)), dma((2,)), dma, dma,
                dma((sections, chunks)), dma((sections, chunks)),
            ],
            compiler_params=pltpu.CompilerParams(collective_id=0, has_side_effects=True),
        )(raw_pulses, azimuth_taps, range_taps, steering, angle_mats,
          range_resampler_matrices, beam_phase, tap_blocks)

    return jax.shard_map(
        local,
        mesh=mesh,
        in_specs=(P(None, "pulse", "rng"), P(), P(), P(), P(), P(), P(), P(None, None, "rng")),
        out_specs=P(None, "pulse", "rng"),
        check_vma=False,
    )
```

time: 125 us -> 68.5 us (0.55); the launches traced: 122 us -> 68.3 us
  Pallas kernels: 0 us -> 66.4 us
  waiting for transfers between devices: 47.8 us -> 0 us
  other arithmetic: 31.9 us -> 0 us
  matrix products: 17.1 us -> 0 us
  local copies, waits for them, and re-layouts: 13.3 us -> 1.87 us
  starting transfers between devices: 11.2 us -> 0 us
    pallas_call x0 -> x1, Pallas kernels: none -> 66.4 us  [local(): pl.pallas_call(functools.partial(kernel, n, nr), out_shape=jax.ShapeDtype...]
    ppermute x7 -> x0, waiting for transfers between devices: 47.8 us -> none  [the longest x4 43.8 us: swapped(): return lax.ppermute(value, axis, pairs)]
    another operation x19 -> x0, other arithmetic: 28.6 us -> none
    dot_general x23 -> x0, matrix products: 17.1 us -> none  [the longest x8 6.23 us: resample(): jnp.einsum('kcani,kij->canj', picked, range_pair, preferred_element_type=...]
    ppermute x7 -> x0, starting transfers between devices: 11.2 us -> none  [the longest x4 4.16 us: swapped(): return lax.ppermute(value, axis, pairs)]
    slice x16 -> x0, local copies, waits for them, and re-layouts: 6.29 us -> none  [the longest x8 2.96 us: resample(): moved[0] * cosine - moved[1] * sine]
    squeeze x16 -> x0, local copies, waits for them, and re-layouts: 4.7 us -> none  [the longest x8 3.91 us: resample(): moved[0] * cosine - moved[1] * sine]
    convert_element_type x3 -> x0, other arithmetic: 2.1 us -> none  [the longest x2 1.18 us: azimuth(): lax.slice_in_dim(padded, offset, offset + count, axis=1).astype(jnp.float32)]
  transfers between devices with their start and end apart: 7 -> 0, of which waited for: 5 -> 0; matrix products, arithmetic and copies ran while one was open for 14% -> 0% of each run, Pallas kernels for 0% -> 0%
where the time goes in v1:
time: 68.5 us; the launch traced here: 68.3 us
  Pallas kernels  66.4 us (97%)
  local copies, waits for them, and re-layouts  1.87 us (3%)
    pallas_call x1, Pallas kernels, local(): pl.pallas_call(functools.partial(kernel, n, nr), out_shape=jax.ShapeDtype...  66.4 us
    unnamed x1, local copies, waits for them, and re-layouts  1.87 us

profile of v1, /device:TPU:6, one launch (start us, length us, event | category | flops | bytes accessed | tf_op | source)
XLA Modules:
  0.0 68.3 jit_solution(14066788014213444783)
XLA Ops:
  0.0 66.4 %shard_map.82 = bf16[2,32,4096]{2,1,0:T(8,128)(2,1)} custom-call(bf16[2,32,4096]{2,1,0:T(8,128)(2,1)} %raw.1, f32[2,9]{1,0:T(2,128)} %az.1, bf16[2,128]{1,0:T(2,128)(2,1)} %rt.1, bf16[2,32,32]{2,1,0:T(8,128)(2,1)} %st.1, bf16[4,2,32,32]{3,2,1,0:T(8,128)(2,1)} %am.1, bf16[4,2,128,128]{3,2,1,0:T(8,128)(2,1)} %rr.1, f32[4,64]{1,0:T(4,128)} %bp.1, s32[4,2,32]{2,1,0:T(2,128)} %tb.1), custom_call_target="tpu_custom_call" | custom-call | tf_op jit(solution)/shard_map/pallas_call | solution.py:288
  66.5 1.9 %copy.10 = bf16[2,32,4096]{2,1,0:T(8,128)(2,1)} copy(bf16[2,32,4096]{2,1,0:T(8,128)(2,1)} %shard_map.82) | data formatting | bytes 1048576

commit v2 on v1

--- a/solution.py
+++ b/solution.py
@@ -58,7 +58,7 @@
 
 
 def kernel(n, nr, raw, az, rt, st, am, rr, bp, tb, out,
-           edge_out, edge_in, rim_out, rim_in, filt, x, turned, sendb, recvb, own, cs, w,
+           edge_out, edge_in, rim_out, rim_in, filt, held, far, near, turned, late, message, own, duals, singles, w,
            edge_send, edge_recv, rim_send, rim_recv, send_sem, recv_sem):
     me, rn = lax.axis_index("pulse"), lax.axis_index("rng")
     count, bins = raw.shape[1], raw.shape[2]
@@ -66,7 +66,8 @@
     blocks = bins // width
     half = az.shape[1] // 2
     sections = n.bit_length() - 1
-    chunks = sendb.shape[1]
+    chunks = held.shape[1]
+    plain = sections - 3
     span = bins // chunks
     per = span // width
 
@@ -135,16 +136,39 @@
         w[(2 * e + 1) * width : (2 * e + 2) * width, :width] = (-m1).astype(BF16)
         w[(2 * e + 1) * width : (2 * e + 2) * width, width:] = m0.astype(BF16)
     beams = am.shape[2]
-    for s in range(sections):
-        parity = (me // 2**s) % 2
-        sign = (2 * parity - 1).astype(F32)
-        for i, sector in enumerate((1 - parity, parity)):
-            phases = jnp.broadcast_to(bp[s : s + 1, :], (beams, 2 * beams))
-            hit = iota((beams, 2 * beams), 1) == iota((beams, 2 * beams), 0) + sector * beams
-            angle = sign * jnp.sum(jnp.where(hit, phases, 0.0), axis=1, keepdims=True)
-            angle = jnp.broadcast_to(angle, (beams, width))
-            cs[s, i, 0] = jnp.cos(angle)
-            cs[s, i, 1] = jnp.sin(angle)
+
+    def parity(s):
+        return (me // 2**s) % 2
+
+    def turning(s, sector, terms):
+        columns = 2 * 2 * beams * terms
+        sign = (2 * parity(s) - 1).astype(F32)
+        phases = jnp.broadcast_to(bp[s : s + 1, :], (beams, 2 * beams))
+        hit = iota((beams, 2 * beams), 1) == iota((beams, 2 * beams), 0) + sector * beams
+        angle = sign * jnp.sum(jnp.where(hit, phases, 0.0), axis=1, keepdims=True)
+        angle = jnp.broadcast_to(angle, (beams, 128))
+        cosine, sine = jnp.cos(angle)[:, :1], jnp.sin(angle)[:, :1]
+        beam, column = iota((beams, columns), 0), iota((beams, columns), 1)
+        real, imag, other = (jnp.zeros((beams, columns), jnp.bool_) for _ in range(3))
+        for k in range(2 * terms):
+            base = 2 * beams * k
+            real = real | (column == beam + base)
+            imag = imag | (column == beam + base + beams)
+            if k % terms == 1:
+                other = other | ((column >= base) & (column < base + 2 * beams))
+        matrix = am[s, sector]
+        on_real = mm(matrix, real.astype(BF16))
+        on_imag = mm(matrix, imag.astype(BF16))
+        turn = jnp.where(other, -sine, sine)
+        whole = jnp.concatenate([cosine * on_real - turn * on_imag, turn * on_real + cosine * on_imag], axis=0)
+        lead = whole.astype(BF16).astype(F32)
+        return jnp.where(iota(whole.shape, 1) < columns // 2, lead, whole - lead).astype(BF16)
+
+    for s in range(plain + 1):
+        duals[s] = turning(s, parity(s), 2)
+    singles[0] = turning(plain + 1, 1 - parity(plain + 1), 1)
+    singles[1] = turning(plain + 1, parity(plain + 1), 1)
+    duals[plain + 1] = turning(plain + 2, parity(plain + 2), 2)
 
     @pl.when(me == 0)
     def _():
@@ -190,6 +214,20 @@
         to_right.wait_recv()
         filt[:, :count, :] = rim_in[...]
 
+    copies = []
+
+    def send(source, target, kind, c, s):
+        copy = pltpu.make_async_remote_copy(
+            source, target, send_sem.at[kind, c], recv_sem.at[kind, c],
+            device_id=(partner(s), rn), device_id_type=MESH)
+        copy.start()
+        return copy
+
+    def arrived(target, kind, c):
+        pltpu.make_async_remote_copy(
+            target, target, send_sem.at[kind, c], recv_sem.at[kind, c],
+            device_id=(partner(0), rn), device_id_type=MESH).wait_recv()
+
     weights = w[...]
     for c in range(chunks):
         r0 = c * per * count
@@ -199,63 +237,89 @@
              filt[0, r0:r1, :], filt[1, r0:r1, :]], axis=1)
         res = mm(lhs, weights).astype(BF16)
         for j in range(per):
-            b = c * per + j
             for part in range(2):
-                x[part * count : (part + 1) * count, b * width : (b + 1) * width] = res[
+                held[0, c, part * count : (part + 1) * count, j * width : (j + 1) * width] = res[
                     j * count : (j + 1) * count, part * width : (part + 1) * width]
+        if plain:
+            copies.append(send(held.at[0, c], near.at[0, c], 0, c, 0))
 
     start = rn * blocks
-    for s in range(sections):
-        parity = (me // 2**s) % 2
-        sectors = (1 - parity, parity)
-        a_out, a_own = am[s, 1 - parity], am[s, parity]
-        a2 = jnp.concatenate([mm(a_out, p0), mm(a_out, p1), mm(a_own, p0), mm(a_own, p1)], axis=0).astype(BF16)
+
+    def turn(matrix, sources, c):
+        parts = [source[c] for source in sources]
+        value = mm(matrix, jnp.concatenate(parts + parts, axis=0)).astype(BF16)
+        for j in range(per):
+            turned[c * per + j] = value[:, j * width : (j + 1) * width]
+
+    def move(s, sector, c):
+        pair = jnp.concatenate([rr[s, 0], rr[s, 1]], axis=0)
+        lhs = []
+        for j in range(per):
+            t = jnp.maximum(tb[s, sector, c * per + j] - start, 0)
+            lhs.append(jnp.concatenate([turned[t], turned[t + 1]], axis=1))
+        res = mm(jnp.concatenate(lhs, axis=0), pair)
+        return jnp.concatenate([res[2 * j * beams : 2 * (j + 1) * beams] for j in range(per)], axis=1)
+
+    def apply(matrix, sources, s, sector, target, then=None):
         for c in range(chunks):
-            value = mm(a2, x[:, c * span : (c + 1) * span]).astype(BF16)
-            for j in range(per):
-                for i in range(2):
-                    turned[i, c * per + j] = value[
-                        i * 2 * beams : (i + 1) * 2 * beams, j * width : (j + 1) * width]
-        pair = jnp.concatenate([rr[s, 0], rr[s, 1]], axis=0)
-
-        def moved(i, c):
-            lhs = []
-            for j in range(per):
-                t = jnp.maximum(tb[s, sectors[i], c * per + j] - start, 0)
-                lhs.append(jnp.concatenate([turned[i, t], turned[i, t + 1]], axis=1))
-            res = mm(jnp.concatenate(lhs, axis=0), pair)
-            cosine, sine = cs[s, i, 0], cs[s, i, 1]
-            for j in range(per):
-                re = res[2 * j * beams : (2 * j + 1) * beams]
-                im = res[(2 * j + 1) * beams : (2 * j + 2) * beams]
-                yield j, re * cosine - im * sine, re * sine + im * cosine
-
-        copies = []
+            turn(matrix, sources, c)
         for c in range(chunks):
-            for j, re, im in moved(0, c):
-                sendb[s, c, :beams, j * width : (j + 1) * width] = re.astype(BF16)
-                sendb[s, c, beams:, j * width : (j + 1) * width] = im.astype(BF16)
-            copy = pltpu.make_async_remote_copy(
-                sendb.at[s, c], recvb.at[s, c], send_sem.at[s, c], recv_sem.at[s, c],
-                device_id=(partner(s), rn), device_id_type=MESH)
-            copy.start()
-            copies.append(copy)
+            target[c] = move(s, sector, c).astype(target.dtype)
+            if then is not None:
+                then(c)
+
+    k, y, z, yz = plain, plain, plain + 1, plain + 2
+
+    def pass_on(s, c):
+        copies.append(send(held.at[s, c], near.at[s, c], s, c, s))
+
+    def to_far(c):
+        copies.append(send(held.at[k, c], far.at[0, c], z, c, k + 2))
+        pass_on(k, c)
+
+    for s in range(plain):
         for c in range(chunks):
-            for j, re, im in moved(1, c):
-                b = c * per + j
-                own[:beams, b * width : (b + 1) * width] = re
-                own[beams:, b * width : (b + 1) * width] = im
+            arrived(near.at[s, c], s, c)
+        follow = to_far if s + 1 == plain else functools.partial(pass_on, s + 1)
+        apply(duals[s], (held.at[s], near.at[s]), s, parity(s), held.at[s + 1], follow)
+    if not plain:
         for c in range(chunks):
-            copies[c].wait_recv()
-            cols = slice(c * span, (c + 1) * span)
-            merged = (own[:, cols] + recvb[s, c].astype(F32)).astype(BF16)
-            if s == sections - 1:
-                out[0, :, cols] = merged[:beams]
-                out[1, :, cols] = merged[beams:]
-            else:
-                x[:, cols] = merged
-        for copy in copies:
-            copy.wait_send()
+            to_far(c)
+
+    def relay(c):
+        arrived(far.at[0, c], z, c)
+        copies.append(send(far.at[0, c], far.at[1, c], yz, c, k))
+
+    early = chunks // 2
+    for c in range(early):
+        relay(c)
+    for c in range(chunks):
+        arrived(near.at[k, c], y, c)
+    apply(duals[k], (held.at[k], near.at[k]), k, parity(k), late.at[0])
+    for c in range(early, chunks):
+        relay(c)
+    out_half, own_half = 1 - parity(k + 1), parity(k + 1)
+    apply(singles[0], (late.at[0],), k + 1, out_half, late.at[2])
+    for c in range(chunks):
+        arrived(far.at[1, c], yz, c)
+    apply(duals[k], (far.at[0], far.at[1]), k, parity(k), late.at[1])
+    apply(singles[0], (late.at[1],), k + 1, out_half, late.at[3])
+
+    def deliver(c):
+        copies.append(send(message.at[0, c], message.at[1, c], plain + 3, c, k + 1))
+
+    apply(duals[k + 1], (late.at[2], late.at[3]), k + 2, parity(k + 2), message.at[0], deliver)
+    apply(singles[1], (late.at[0],), k + 1, own_half, late.at[2])
+    apply(singles[1], (late.at[1],), k + 1, own_half, late.at[3])
+    apply(duals[k + 1], (late.at[2], late.at[3]), k + 2, parity(k + 2), own)
+    for c in range(chunks):
+        arrived(message.at[1, c], plain + 3, c)
+        merged = (own[c] + message[1, c].astype(F32)).astype(BF16)
+        cols = slice(c * span, (c + 1) * span)
+        out[0, :, cols] = merged[:beams]
+        out[1, :, cols] = merged[beams:]
+    for copy in copies:
+        copy.wait_send()
 
     @pl.when(me > 0)
     def _():
@@ -280,8 +344,10 @@
         half = azimuth_taps.shape[1] // 2
         blocks = bins // width
         sections = n.bit_length() - 1
-        chunks = 4
+        chunks = 8
+        plain = sections - 3
         rows = 2 * count
+        image = (chunks, rows, bins // chunks)
         vmem = pl.BlockSpec(memory_space=pltpu.VMEM)
         smem = pl.BlockSpec(memory_space=pltpu.SMEM)
         dma = pltpu.SemaphoreType.DMA
@@ -296,15 +362,18 @@
                 pltpu.VMEM((2, count, width), BF16),
                 pltpu.VMEM((2, count, width), BF16),
                 pltpu.VMEM((2, (blocks + 1) * count, width), BF16),
-                pltpu.VMEM((rows, bins), BF16),
-                pltpu.VMEM((2, blocks, rows, width), BF16),
-                pltpu.VMEM((sections, chunks, rows, bins // chunks), BF16),
-                pltpu.VMEM((sections, chunks, rows, bins // chunks), BF16),
-                pltpu.VMEM((rows, bins), F32),
-                pltpu.VMEM((sections, 2, 2, count, width), F32),
+                pltpu.VMEM((plain + 1, *image), BF16),
+                pltpu.VMEM((2, *image), BF16),
+                pltpu.VMEM((plain + 1, *image), BF16),
+                pltpu.VMEM((blocks, rows, width), BF16),
+                pltpu.VMEM((4, *image), BF16),
+                pltpu.VMEM((2, *image), BF16),
+                pltpu.VMEM(image, F32),
+                pltpu.VMEM((plain + 2, rows, 4 * rows), BF16),
+                pltpu.VMEM((2, rows, 2 * rows), BF16),
                 pltpu.VMEM((4 * width, 2 * width), BF16),
                 dma((2,)), dma((2,)), dma, dma,
-                dma((sections, chunks)), dma((sections, chunks)),
+                dma((plain + 4, chunks)), dma((plain + 4, chunks)),
             ],
             compiler_params=pltpu.CompilerParams(collective_id=0, has_side_effects=True),
         )(raw_pulses, azimuth_taps, range_taps, steering, angle_mats,

time: 68.5 us -> 59.2 us (0.86); the launches traced: 68.3 us -> 58 us
  Pallas kernels: 66.4 us -> 56.2 us
    pallas_call x1, Pallas kernels: 66.4 us -> 56.2 us  [local(): pl.pallas_call(functools.partial(kernel, n, nr), out_shape=jax.ShapeDtype...]
where the time goes in v2:
time: 59.2 us; the launch traced here: 58 us
  Pallas kernels  56.2 us (95%)
  local copies, waits for them, and re-layouts  1.87 us (3%)
    pallas_call x1, Pallas kernels, local(): pl.pallas_call(functools.partial(kernel, n, nr), out_shape=jax.ShapeDtype...  56.2 us
    unnamed x1, local copies, waits for them, and re-layouts  1.87 us

profile of v2, /device:TPU:6, one launch (start us, length us, event | category | flops | bytes accessed | tf_op | source)
XLA Modules:
  0.0 58.0 jit_solution(5427436684041958314)
XLA Ops:
  0.0 56.2 %shard_map.82 = bf16[2,32,4096]{2,1,0:T(8,128)(2,1)} custom-call(bf16[2,32,4096]{2,1,0:T(8,128)(2,1)} %raw.1, f32[2,9]{1,0:T(2,128)} %az.1, bf16[2,128]{1,0:T(2,128)(2,1)} %rt.1, bf16[2,32,32]{2,1,0:T(8,128)(2,1)} %st.1, bf16[4,2,32,32]{3,2,1,0:T(8,128)(2,1)} %am.1, bf16[4,2,128,128]{3,2,1,0:T(8,128)(2,1)} %rr.1, f32[4,64]{1,0:T(4,128)} %bp.1, s32[4,2,32]{2,1,0:T(2,128)} %tb.1), custom_call_target="tpu_custom_call" | custom-call | tf_op jit(solution)/shard_map/pallas_call | solution.py:354
  56.2 1.9 %copy.10 = bf16[2,32,4096]{2,1,0:T(8,128)(2,1)} copy(bf16[2,32,4096]{2,1,0:T(8,128)(2,1)} %shard_map.82) | data formatting | bytes 1048576
